TPU v7x, 32 devices: a whole 2x2x4 slice. The times are simulated.
32 devices in a mesh: grp: 2 (over y), row: 4 (over x, core), col: 4 (over z).
Axes of the slice: x: 2, y: 2, z: 4, core: 2. Of those that a mesh axis runs over, the one named last changes fastest.
Arguments:
- sigma_anc: float32 [1536, 768], P(('grp', 'row'), 'col'), parts along dimension 0, may hold values from -3 to 23, as said below
- anc_factor: float32 [1536, 2, 512], P(('grp', 'row', 'col')), parts along dimension 0, may hold values from -0.625 to 0.625
- diag_inverse: float32 [4, 512, 512], P('grp', None, 'row'), parts along dimension 0, may hold values from -0.6 to 1.5, as said below
- pattern: int32 [2, 6], replicated, may hold values from 0 to 1, as said below
Outputs:
- sel_off: float32 [1536, 2, 512], P(('grp', 'row', 'col')), parts along dimension 0
- sel_diag: float32 [4, 512, 512], P('grp'), parts along dimension 0
There are 2 independent parts, one for each index of `grp`. A program takes and returns all parts, laid end to end along the dimension named above; an argument that names none is the same for every part. Nothing has to cross between parts.
Inputs may be any that keep to these rules, and one draw needn't show every extreme that they name: `pattern`: each supernode's present row blocks are a run of consecutive blocks, wrapping around the end, of at least 0 blocks, at most 3, together with some scattered others. `sigma_anc`: symmetric and positive definite. `diag_inverse`: lower triangular, with diagonal entries between 0.5 and 1.5 and small entries below the diagonal.
All inputs are finite; a program needn't handle non-finite values.
Results may differ from a plain program's by a relative error of at most 0.00013.
Values sent between devices are 32-bit elements; how exact they have to be, the bound alone decides.
A program may use at most 64 MiB of HBM per device.

v0:
```python
import jax
import jax.numpy as jnp
from jax import lax
from jax.sharding import PartitionSpec as P


def body(sigma_anc, anc_factor, diag_inverse, pattern):
    precise = lax.Precision.HIGHEST
    rows_dev, supers, super_width = anc_factor.shape
    row_count = lax.axis_size("row")
    col_count = lax.axis_size("col")
    position = lax.axis_index("row") * col_count + lax.axis_index("col")
    total_rows = rows_dev * row_count * col_count
    block_size = total_rows // pattern.shape[1]
    flat_mask = jnp.repeat(pattern.astype(jnp.float32), block_size, axis=1)
    own_mask = jnp.transpose(lax.dynamic_slice_in_dim(flat_mask, position * rows_dev, rows_dev, 1))[
        :, :, None
    ]
    device_total = row_count * col_count
    share = -(-super_width // device_total)
    masked_factor = anc_factor * own_mask
    flattened = masked_factor.reshape(rows_dev, -1)
    gathered = lax.all_gather(flattened, "row", axis=0, tiled=True)
    stacked = gathered.reshape(row_count, rows_dev, flattened.shape[1])
    turned = lax.all_to_all(stacked, "col", split_axis=0, concat_axis=1, tiled=True)
    column_block = turned.reshape(row_count * rows_dev, flattened.shape[1])
    summed_rows = lax.psum_scatter(
        jnp.dot(sigma_anc, column_block, precision=precise, preferred_element_type=jnp.float32),
        "col",
        scatter_dimension=0,
        tiled=True,
    )
    off_factor = -(summed_rows.reshape(masked_factor.shape) * own_mask)
    both_rows = jnp.concatenate([masked_factor, off_factor], axis=0)
    column_piece = lax.all_gather(diag_inverse, "row", axis=2, tiled=True)
    product = jnp.einsum("rsk,skj->rsj", both_rows, column_piece, precision=precise)
    own_rows = lax.dynamic_slice_in_dim(column_piece, position * share, share, 1)
    scaled = product[:rows_dev]
    sel_off = product[rows_dev:]
    diag_term = jnp.einsum("skj,skl->sjl", own_rows, own_rows, precision=precise)
    partial_value = diag_term - jnp.einsum("rsj,rsl->sjl", scaled, sel_off, precision=precise)
    sel_diag = lax.psum(partial_value, ("row", "col"))
    return (sel_off, sel_diag)


def solution(mesh):
    return jax.shard_map(
        body,
        mesh=mesh,
        in_specs=(
            P(("grp", "row"), "col"),
            P(("grp", "row", "col"), None, None),
            P("grp", None, "row"),
            P(),
        ),
        out_specs=(P(("grp", "row", "col"), None, None), P("grp", None, None)),
        check_vma=False,
    )
```

profile of v0, /device:TPU:9, one launch (start us, length us, event | category | flops | bytes accessed | tf_op | source)
XLA Modules:
  0.0 184.3 jit_solution(452743404980939759)
XLA Ops:
  8.0 0.0 copy-start
  8.0 0.0 reduce-scatter.2.cloned.1.call-start
  8.1 0.7 convert_element_type.3
  8.8 0.1 broadcast_bitcast_fusion
  8.9 0.1 dynamic-slice_bitcast_fusion
  8.9 1.0 fusion.13
  10.0 9.1 %all_gather.6 = f32[192,1024]{1,0:T(8,128)S(1)} all-gather(f32[48,1024]{1,0:T(8,128)S(1)} %bitcast.26), channel_id=1, replica_groups=mesh['grp'=2,'row'=4,'col'=4] {'row'}, dimensions={0}, use_global_device_ids=true | all-gather | bytes 983040 | tf_op jit(solution)/shard_map/all_gather | solution.py:23
  19.1 0.0 copy-start.2
  19.1 22.6 %all_to_all.4 = f32[4,48,1024]{2,1,0:T(8,128)S(1)} all-to-all(f32[4,48,1024]{2,1,0:T(8,128)S(1)} %bitcast.25), channel_id=1, replica_groups=mesh['grp'=2,'row'=4,'col'=4] {'col'}, dimensions={0} | all-to-all | bytes 1572864 | tf_op jit(solution)/shard_map/all_to_all | solution.py:25
  41.7 0.0 copy-done
  41.7 1.7 convolution_bitcast_fusion
  43.4 0.0 reduce-scatter.2.cloned.1.call-update
  43.4 0.0 all-gather.2.cloned.1.call-start
  43.5 0.5 all-gather.2.cloned.1.call-update
  44.0 0.0 all-reduce.2.cloned.1.call-start
  44.0 0.0 copy-done.2
  44.1 0.1 copy_multiply_fusion
  44.1 21.3 %reduce-scatter.2.cloned.1.call-done = f32[48,1024]{1,0:T(8,128)} async-done(((f32[192,1024]{1,0:T(8,128)}), f32[48,1024]{1,0:T(8,128)}) %reduce-scatter.2.cloned.1.call-update) | async-done | bytes 196624 | tf_op jit(solution)/shard_map/reduce_scatter | solution.py:27
  65.5 1.0 fusion.3
  66.5 3.0 %all-gather.2.cloned.1.call-done = f32[2,512,512]{2,1,0:T(8,128)} async-done(((f32[2,512,128]{2,1,0:T(8,128)}), f32[2,512,512]{2,1,0:T(8,128)}) %all-gather.2.cloned.1.call-update) | async-done | bytes 2097168 | tf_op jit(solution)/shard_map/all_gather | solution.py:35
  69.5 0.0 copy-start.1
  69.5 3.0 %fusion.5 = f32[2,512,512]{2,1,0:T(8,128)S(1)} fusion(f32[2,512,512]{2,1,0:T(8,128)} %all-gather.2.cloned.1.call-done, s32[]{:T(128)S(6)} %select_n.7), kind=kOutput, calls=%fused_computation.10 | convolution fusion | flops 201326592 | bytes 2228228 | tf_op jit(solution)/shard_map/skj,skl->sjl/dot_general | solution.py:40
  72.5 0.0 copy-done.1
  72.5 1.3 convolution_bitcast_fusion.1
  73.8 3.2 %convolution_subtract_fusion = f32[2,512,512]{2,1,0:T(8,128)} fusion(f32[2,512,512]{2,1,0:T(8,128)S(1)} %fusion.5, f32[96,2,512]{2,0,1:T(8,128)S(1)} %convolution_bitcast_fusion.1), kind=kOutput, calls=%fused_computation | convolution fusion | flops 302514176 | bytes 4587520 | tf_op jit(solution)/shard_map/rsj,rsl->sjl/dot_general | solution.py:41
  77.0 0.0 all-reduce.2.cloned.1.call-update
  77.0 0.8 copy.12
  77.9 95.9 %all-reduce.2.cloned.1.call-done = f32[2,512,512]{2,1,0:T(8,128)} async-done(((f32[2,512,512]{2,1,0:T(8,128)}), f32[2,512,512]{2,1,0:T(8,128)}) %all-reduce.2.cloned.1.call-update) | async-done | bytes 2097168 | tf_op jit(solution)/shard_map/psum | solution.py:42
  173.7 3.1 %copy.23 = f32[2,512,512]{2,1,0:T(8,128)} copy(f32[2,512,512]{2,1,0:T(8,128)} %all-reduce.2.cloned.1.call-done) | data formatting | bytes 4194304
  (3 shorter events, 0.0 us)
Async XLA Ops:
  8.0 33.7 %copy-start = (f32[192,192]{1,0:T(8,128)S(1)}, f32[192,192]{1,0:T(8,128)}, u32[]{:S(2)}) copy-start(f32[192,192]{1,0:T(8,128)} %param.4) | copy-start | bytes 442372
  8.0 57.5 %reduce-scatter.2.cloned.1.call-start = ((), (), s32[]{:S(2)}) async-start(), calls=%async_computation.2 | async-start | bytes 983040 | tf_op jit(solution)/shard_map/reduce_scatter | solution.py:27
  19.1 25.0 %copy-start.2 = (f32[48,2,512]{2,1,0:T(2,128)S(1)}, f32[48,2,512]{2,1,0:T(2,128)}, u32[]{:S(2)}) copy-start(f32[48,2,512]{2,1,0:T(2,128)} %param.5) | copy-start | bytes 589828
  43.4 26.1 %all-gather.2.cloned.1.call-start = ((), (), s32[]{:S(2)}) async-start(), calls=%async_computation.3 | async-start | bytes 2621440 | tf_op jit(solution)/shard_map/all_gather | solution.py:35
  44.0 129.7 %all-reduce.2.cloned.1.call-start = ((), (), s32[]{:S(2)}) async-start(), calls=%async_computation.4 | async-start | bytes 4194304 | tf_op jit(solution)/shard_map/psum | solution.py:42
  69.5 3.0 %copy-start.1 = (f32[2,512,512]{2,1,0:T(8,128)S(1)}, f32[2,512,512]{2,1,0:T(8,128)}, u32[]{:S(2)}) copy-start(f32[2,512,512]{2,1,0:T(8,128)} %all-gather.2.cloned.1.call-done) | copy-start | bytes 6291460
Sparse Core Ops, SparseCore 0:
  43.5 21.8 reduce-scatter.1
  77.1 96.5 all-reduce.1
Sparse Core Ops, SparseCore 1:
  45.4 24.0 all-gather.1
where the time goes:
time: 187 us; the launch traced here: 184 us
  waiting for transfers between devices  121 us (65%)
  blocking collectives  31.7 us (17%)
  between operations  15.6 us (8%)
  matrix products  9.2 us (5%)
  local copies, waits for them, and re-layouts  4.11 us (2%)
  other arithmetic  2.82 us (2%)
    psum x1, waiting for transfers between devices, body(): sel_diag = lax.psum(partial_value, ('row', 'col'))  95.9 us
    all_to_all x1, blocking collectives, body(): lax.all_to_all(stacked, 'col', split_axis=0, concat_axis=1, tiled=True)  22.6 us
    reduce_scatter x1, waiting for transfers between devices, body(): lax.psum_scatter(jnp.dot(sigma_anc, column_block, precision=precise, pref...  21.3 us
    all_gather x1, blocking collectives, body(): gathered = lax.all_gather(flattened, 'row', axis=0, tiled=True)  9.11 us
    unnamed x10, local copies, waits for them, and re-layouts  4.01 us
  transfers between devices with their start and end apart: 3, of which 3 were waited for; matrix products, arithmetic and copies ran while one was open for 1% of the time, Pallas kernels for 0%

commit v1 on v0

--- a/solution.py
+++ b/solution.py
@@ -1,10 +1,392 @@
+import functools
+
 import jax
 import jax.numpy as jnp
 from jax import lax
+from jax.experimental import pallas as pl
+from jax.experimental.pallas import tpu as pltpu
 from jax.sharding import PartitionSpec as P
 
-
-def body(sigma_anc, anc_factor, diag_inverse, pattern):
+LANES = 128
+SUBLANES = 8
+
+
+def split(x):
+    high = x.astype(jnp.bfloat16)
+    low = (x - high.astype(jnp.float32)).astype(jnp.bfloat16)
+    return high, low
+
+
+def dot3(a, b, contract=((1,), (0,))):
+    (ah, al), (bh, bl) = a, b
+    f = lambda u, v: lax.dot_general(u, v, (contract, ((), ())), preferred_element_type=jnp.float32)
+    return f(ah, bh) + (f(ah, bl) + f(al, bh))
+
+
+def fused_kernel(
+    n_r, n_c, supers, width, rows_dev, block_size,
+    sig_ref, a_ref, d_ref, pat_ref,
+    off_ref, diag_ref,
+    ag, ta, dfull, pbuf, rbuf, sbuf, rbuf2, left, right, goth, gown, grecv, hx, hrecv, zs, zrecv, res, tout, toff,
+    send_sems, s_ag, s_ta, s_d, s_p, s_p2, s_g, s_h, s_z, s_zag, s_xag, s_sib, s_off, local_sems,
+):
+    r = lax.axis_index("row")
+    c = lax.axis_index("col")
+    n_x = n_r // 2
+    x = r // 2
+    k = r % 2
+    sib = 2 * x + 1 - k
+    piece = width // n_r
+    nb = width // LANES
+    half_rows = nb * (nb + 1) // 2 * LANES
+    q = half_rows // (n_x * n_c)
+    share = width // (n_r * n_c)
+    block_rows = rows_dev * n_c
+    sends = []
+
+    def rcopy(src, dst, rsem, row, col):
+        cp = pltpu.make_async_remote_copy(
+            src_ref=src, dst_ref=dst, send_sem=send_sems.at[len(sends)], recv_sem=rsem,
+            device_id={"row": row, "col": col}, device_id_type=pl.DeviceIdType.MESH,
+        )
+        cp.start()
+        sends.append(cp)
+
+    def wait_recv(dst, rsem):
+        pltpu.make_async_copy(dst, dst, rsem).wait()
+
+    barrier = pltpu.get_barrier_semaphore()
+    sig = lambda row, col: pl.semaphore_signal(
+        barrier, inc=1, device_id={"row": row, "col": col}, device_id_type=pl.DeviceIdType.MESH
+    )
+    for dc in range(1, n_c):
+        sig(r, (c + dc) % n_c)
+    sig(sib, c)
+    for dx in range(1, n_x):
+        sig(2 * ((x + dx) % n_x) + k, c)
+
+    @pl.when(r != c)
+    def _():
+        sig(c, r)
+        pl.semaphore_wait(barrier, n_c + n_x)
+
+    @pl.when(r == c)
+    def _():
+        pl.semaphore_wait(barrier, n_c + n_x - 1)
+
+    for dc in range(1, n_c):
+        rcopy(a_ref, ag.at[c], s_ag.at[c], r, (c + dc) % n_c)
+    d_slice = lambda ref, rr: ref.at[:, pl.ds(rr * piece, width - rr * piece), pl.ds(rr * piece, piece)]
+    d_src = lambda rr: d_ref.at[:, pl.ds(rr * piece, width - rr * piece), :]
+
+    def d_copy(src, rr, slot, row):
+        return pltpu.make_async_remote_copy(
+            src_ref=src, dst_ref=d_slice(dfull, rr), send_sem=send_sems.at[slot], recv_sem=s_d.at[rr],
+            device_id={"row": row, "col": c}, device_id_type=pl.DeviceIdType.MESH,
+        )
+
+    n_fixed = 64
+    for rr in range(n_r):
+        @pl.when(r == rr)
+        def _():
+            for dx in range(1, n_x):
+                d_copy(d_src(rr), rr, n_fixed + dx, 2 * ((x + dx) % n_x) + k).start()
+            d_copy(d_src(rr), rr, n_fixed, sib).start()
+            pltpu.make_async_copy(d_src(rr), d_slice(dfull, rr), local_sems.at[0]).start()
+    own_copy = pltpu.make_async_copy(a_ref, ag.at[c], local_sems.at[1])
+    own_copy.start()
+
+    def ta_copy():
+        return pltpu.make_async_remote_copy(
+            src_ref=a_ref, dst_ref=ta, send_sem=send_sems.at[n_fixed - 1], recv_sem=s_ta.at[0],
+            device_id={"row": c, "col": r}, device_id_type=pl.DeviceIdType.MESH,
+        )
+
+    ta_local = lambda: pltpu.make_async_copy(a_ref, ta, s_ta.at[0])
+
+    @pl.when(r != c)
+    def _():
+        ta_copy().start()
+
+    @pl.when(r == c)
+    def _():
+        ta_local().start()
+
+    for rr in range(1, n_r):
+        dfull[:, 0 : rr * piece, rr * piece : (rr + 1) * piece] = jnp.zeros((supers, rr * piece, piece), jnp.float32)
+
+    def mask_of(first, rows, s):
+        row = first + lax.broadcasted_iota(jnp.int32, (rows, 1), 0)
+        m = jnp.zeros((rows, 1), jnp.float32)
+        for b in range(pat_ref.shape[1]):
+            inside = (row >= b * block_size) & (row < (b + 1) * block_size)
+            m = jnp.where(inside, pat_ref[s, b].astype(jnp.float32), m)
+        return m
+
+    sigma_t = split(jnp.transpose(sig_ref[...]))
+
+    for rr in range(n_r):
+        @pl.when((rr % 2 == k) & (rr // 2 != x))
+        def _():
+            wait_recv(d_slice(dfull, rr), s_d.at[rr])
+            d_copy(d_slice(dfull, rr), rr, n_fixed + n_x + rr // 2, sib).start()
+
+    own_copy.wait()
+    for dc in range(1, n_c):
+        j = (c + dc) % n_c
+        wait_recv(ag.at[j], s_ag.at[j])
+
+    for s in range(supers):
+        cols = slice(s * width, (s + 1) * width)
+        block = ag[:, :, cols].reshape(block_rows, width) * mask_of(r * block_rows, block_rows, s)
+        part = dot3(sigma_t, split(block))
+        pbuf[:, :, cols] = part.reshape(n_r, rows_dev, width)
+    for i in range(n_x):
+        xo = (x + 1 + i) % n_x
+        rcopy(pbuf.at[2 * xo + 1 - k], rbuf.at[xo], s_p.at[xo], sib, c)
+
+    for rr in range(n_r):
+        @pl.when((rr % 2 != k))
+        def _():
+            wait_recv(d_slice(dfull, rr), s_d.at[rr])
+
+        @pl.when(r == rr)
+        def _():
+            pltpu.make_async_copy(d_src(rr), d_slice(dfull, rr), local_sems.at[0]).wait()
+
+    wait_recv(ta, s_ta.at[0])
+
+    for i in range(n_x):
+        xo = (x + 1 + i) % n_x
+        wait_recv(rbuf.at[xo], s_p.at[xo])
+        sbuf[xo] = pbuf[2 * xo + k] + rbuf[xo]
+        if i < n_x - 1:
+            rcopy(sbuf.at[xo], rbuf2.at[x], s_p2.at[x], 2 * xo + k, c)
+
+    t_first = (c * n_c + r) * rows_dev
+    own_first = (r * n_c + c) * share
+    masks = [mask_of(t_first, rows_dev, s) for s in range(supers)]
+    step = 2 * LANES
+
+    def times_d(rows_value, s, store):
+        for j in range(0, width, step):
+            xs = split(rows_value[:, j:])
+            ds = split(dfull[s, j:, j : j + step])
+            store(j, dot3(xs, ds))
+
+    for s in range(supers):
+        def store_scaled(j, v):
+            left[s, 0:rows_dev, j : j + step] = -v
+        times_d(ta[:, s * width : (s + 1) * width] * masks[s], s, store_scaled)
+        own = dfull[s, pl.ds(pl.multiple_of(own_first, SUBLANES), share), :]
+        left[s, rows_dev:, :] = own
+        right[s, rows_dev:, :] = own
+
+    for dx in range(1, n_x):
+        xo = (x + dx) % n_x
+        wait_recv(rbuf2.at[xo], s_p2.at[xo])
+    for s in range(supers):
+        cols = slice(s * width, (s + 1) * width)
+        y = sbuf[x, :, cols]
+        for dx in range(1, n_x):
+            y = y + rbuf2[(x + dx) % n_x, :, cols]
+        def store_off(j, v):
+            right[s, 0:rows_dev, j : j + step] = v
+            tout[:, s * width + j : s * width + j + step] = v
+        times_d(y * (-masks[s]), s, store_off)
+
+    def diag_part(s, dst):
+        lh, ll = split(left[s])
+        rh, rl = split(right[s])
+        b = 0
+        for i in range(nb):
+            li = slice(i * LANES, (i + 1) * LANES)
+            v = dot3((lh[:, li], ll[:, li]), (rh[:, : (i + 1) * LANES], rl[:, : (i + 1) * LANES]), ((0,), (0,)))
+            for j in range(i + 1):
+                dst[b * LANES : (b + 1) * LANES, :] = v[:, j * LANES : (j + 1) * LANES]
+                b += 1
+
+    diag_part(1 - k, goth)
+    rcopy(goth, grecv, s_g.at[0], sib, c)
+
+    def off_copy():
+        return pltpu.make_async_remote_copy(
+            src_ref=tout, dst_ref=toff, send_sem=send_sems.at[n_fixed - 2], recv_sem=s_off.at[0],
+            device_id={"row": c, "col": r}, device_id_type=pl.DeviceIdType.MESH,
+        )
+
+    off_local = lambda: pltpu.make_async_copy(tout, toff, s_off.at[0])
+
+    diag_part(k, gown)
+    wait_recv(grecv, s_g.at[0])
+
+    rows_at = lambda xo, j: pl.ds(pl.multiple_of((xo * n_c + j) * q, SUBLANES), q)
+    for i in range(n_c):
+        j = (c + 1 + i) % n_c
+        for dx in range(1, n_x):
+            xo = (x + dx) % n_x
+            at = rows_at(xo, j)
+            hx[at, :] = gown[at, :] + grecv[at, :]
+            rcopy(hx.at[at, :], hrecv.at[x, j], s_h.at[x * n_c + j], 2 * xo + k, c)
+    for i in range(n_c):
+        j = (c + 1 + i) % n_c
+        at = rows_at(x, j)
+        v = gown[at, :] + grecv[at, :]
+        for dx in range(1, n_x):
+            xo = (x + dx) % n_x
+            wait_recv(hrecv.at[xo, j], s_h.at[xo * n_c + j])
+            v = v + hrecv[xo, j]
+        zs[j] = v
+        if i < n_c - 1:
+            rcopy(zs.at[j], zrecv.at[c], s_z.at[c], r, j)
+
+    @pl.when(r != c)
+    def _():
+        off_copy().start()
+
+    @pl.when(r == c)
+    def _():
+        off_local().start()
+
+    total = zs[c]
+    for dc in range(1, n_c):
+        j = (c + dc) % n_c
+        wait_recv(zrecv.at[j], s_z.at[j])
+        total = total + zrecv[j]
+    mine = res.at[k, rows_at(x, c), :]
+    res[k, rows_at(x, c), :] = total
+
+    for dc in range(1, n_c):
+        rcopy(mine, mine, s_zag.at[c], r, (c + dc) % n_c)
+    def pass_on(j):
+        chunk = res.at[k, rows_at(x, j), :]
+        for dx in range(1, n_x):
+            rcopy(chunk, chunk, s_xag.at[x * n_c + j], 2 * ((x + dx) % n_x) + k, c)
+        rcopy(chunk, chunk, s_sib.at[x * n_c + j], sib, c)
+    pass_on(c)
+    for dc in range(1, n_c):
+        j = (c + dc) % n_c
+        wait_recv(res.at[k, rows_at(x, j), :], s_zag.at[j])
+        pass_on(j)
+    for dc in range(n_c):
+        j = (c + dc) % n_c
+        for dx in range(1, n_x):
+            xo = (x + dx) % n_x
+            chunk = res.at[k, rows_at(xo, j), :]
+            wait_recv(chunk, s_xag.at[xo * n_c + j])
+            rcopy(chunk, chunk, s_sib.at[xo * n_c + j], sib, c)
+
+    wait_recv(toff, s_off.at[0])
+    off_ref[...] = toff[...]
+
+    def expand(s):
+        b = 0
+        for i in range(nb):
+            for j in range(i + 1):
+                v = res[s, b * LANES : (b + 1) * LANES, :]
+                diag_ref[s, i * LANES : (i + 1) * LANES, j * LANES : (j + 1) * LANES] = v
+                if j < i:
+                    diag_ref[s, j * LANES : (j + 1) * LANES, i * LANES : (i + 1) * LANES] = jnp.transpose(v)
+                b += 1
+
+    expand(k)
+    for xo in range(n_x):
+        for j in range(n_c):
+            wait_recv(res.at[1 - k, rows_at(xo, j), :], s_sib.at[xo * n_c + j])
+    expand(1 - k)
+
+    for cp in sends:
+        cp.wait_send()
+    for rr in range(n_r):
+        @pl.when(r == rr)
+        def _():
+            for dx in range(1, n_x):
+                d_copy(d_src(rr), rr, n_fixed + dx, 2 * ((x + dx) % n_x) + k).wait_send()
+            d_copy(d_src(rr), rr, n_fixed, sib).wait_send()
+
+        @pl.when((rr % 2 == k) & (rr // 2 != x))
+        def _():
+            d_copy(d_slice(dfull, rr), rr, n_fixed + n_x + rr // 2, sib).wait_send()
+
+    @pl.when(r != c)
+    def _():
+        ta_copy().wait_send()
+        off_copy().wait_send()
+
+
+def fused_body(sigma_anc, anc_factor, diag_inverse, pattern):
+    rows_dev, supers, width = anc_factor.shape
+    n_r = lax.axis_size("row")
+    n_c = lax.axis_size("col")
+    n_x = n_r // 2
+    total_rows = rows_dev * n_r * n_c
+    flat = supers * width
+    nb = width // LANES
+    half_rows = nb * (nb + 1) // 2 * LANES
+    q = half_rows // (n_x * n_c)
+    share = width // (n_r * n_c)
+    f32 = lambda *shape: pltpu.VMEM(shape, jnp.float32)
+    dma = lambda n: pltpu.SemaphoreType.DMA((n,))
+    vm = pl.BlockSpec(memory_space=pltpu.VMEM)
+    off, diag = pl.pallas_call(
+        functools.partial(fused_kernel, n_r, n_c, supers, width, rows_dev, total_rows // pattern.shape[1]),
+        out_shape=(
+            jax.ShapeDtypeStruct((rows_dev, flat), jnp.float32),
+            jax.ShapeDtypeStruct((supers, width, width), jnp.float32),
+        ),
+        in_specs=[vm, vm, vm, pl.BlockSpec(memory_space=pltpu.SMEM)],
+        out_specs=(vm, vm),
+        scratch_shapes=[
+            f32(n_c, rows_dev, flat),
+            f32(rows_dev, flat),
+            f32(supers, width, width),
+            f32(n_r, rows_dev, flat),
+            f32(n_x, rows_dev, flat),
+            f32(n_x, rows_dev, flat),
+            f32(n_x, rows_dev, flat),
+            f32(supers, rows_dev + share, width),
+            f32(supers, rows_dev + share, width),
+            f32(half_rows, LANES),
+            f32(half_rows, LANES),
+            f32(half_rows, LANES),
+            f32(half_rows, LANES),
+            f32(n_x, n_c, q, LANES),
+            f32(n_c, q, LANES),
+            f32(n_c, q, LANES),
+            f32(supers, half_rows, LANES),
+            f32(rows_dev, flat),
+            f32(rows_dev, flat),
+            dma(64 + 2 * n_x),
+            dma(n_c), dma(1), dma(n_r), dma(n_x), dma(n_x), dma(1), dma(n_x * n_c), dma(n_c), dma(n_c),
+            dma(n_x * n_c), dma(n_x * n_c), dma(1), dma(2),
+        ],
+        compiler_params=pltpu.CompilerParams(
+            collective_id=0, has_side_effects=True, vmem_limit_bytes=56 * 1024 * 1024
+        ),
+    )(sigma_anc, anc_factor.reshape(rows_dev, flat), diag_inverse, pattern)
+    return off.reshape(anc_factor.shape), diag
+
+
+def fits(sigma_anc, anc_factor, diag_inverse):
+    rows_dev, supers, width = anc_factor.shape
+    n_r = lax.axis_size("row")
+    n_c = lax.axis_size("col")
+    nb = width // LANES
+    chunks = (n_r // 2) * n_c * SUBLANES
+    return (
+        n_r == n_c
+        and n_r % 2 == 0
+        and supers == 2
+        and sigma_anc.shape[0] == sigma_anc.shape[1]
+        and diag_inverse.shape[2] % LANES == 0
+        and width % (2 * LANES) == 0
+        and rows_dev % SUBLANES == 0
+        and width % (n_r * n_c * SUBLANES) == 0
+        and (nb * (nb + 1) // 2 * LANES) % chunks == 0
+    )
+
+
+def plain_body(sigma_anc, anc_factor, diag_inverse, pattern):
     precise = lax.Precision.HIGHEST
     rows_dev, supers, super_width = anc_factor.shape
     row_count = lax.axis_size("row")
@@ -43,6 +425,11 @@
     return (sel_off, sel_diag)
 
 
+def body(sigma_anc, anc_factor, diag_inverse, pattern):
+    run = fused_body if fits(sigma_anc, anc_factor, diag_inverse) else plain_body
+    return run(sigma_anc, anc_factor, diag_inverse, pattern)
+
+
 def solution(mesh):
     return jax.shard_map(
         body,

time: 187 us -> 81.6 us (0.44)
  the two profiles are of different devices: /device:TPU:9 before, /device:TPU:25 now
where the time goes in v1:
time: 81.6 us; the launch traced here: 81.4 us
  Pallas kernels  74.2 us (91%)
  local copies, waits for them, and re-layouts  6.48 us (8%)
    pallas_call x1, Pallas kernels, fused_body(): pl.pallas_call(functools.partial(fused_kernel, n_r, n_c, supers, width, r...  74.2 us
    unnamed x2, local copies, waits for them, and re-layouts  4.72 us
    reshape x1, local copies, waits for them, and re-layouts, fused_body(): return (off.reshape(anc_factor.shape), diag)  1.76 us

profile of v1, /device:TPU:25, one launch (start us, length us, event | category | flops | bytes accessed | tf_op | source)
XLA Modules:
  0.0 81.4 jit_solution(6415312562454930048)
XLA Ops:
  0.6 1.6 %copy.6 = f32[6,8,2,512]{3,1,2,0:T(8,128)} copy(f32[6,8,2,512]{3,2,1,0:T(2,128)} %bitcast.3) | data formatting | bytes 393216
  2.3 74.2 %shard_map.59 = (f32[48,1024]{1,0:T(8,128)}, f32[2,512,512]{2,1,0:T(8,128)}) custom-call(f32[192,192]{1,0:T(8,128)} %sig_ref.1, f32[48,1024]{1,0:T(8,128)} %bitcast.2, f32[2,512,128]{2,1,0:T(8,128)} %d_ref.1, s32[2,6]{1,0:T(2,128)} %pat_ref.1), custom_call_target="tpu_custom_call" | custom-call | tf_op jit(solution)/shard_map/pallas_call | solution.py:331
  76.5 1.8 %reshape.11 = f32[48,2,512]{2,1,0:T(2,128)} reshape(f32[48,1024]{1,0:T(8,128)} %get-tuple-element.4) | data formatting | bytes 393216 | tf_op jit(solution)/shard_map/reshape | solution.py:367
  78.3 3.1 %copy.8 = f32[2,512,512]{2,1,0:T(8,128)} copy(f32[2,512,512]{2,1,0:T(8,128)} %get-tuple-element.9) | data formatting | bytes 4194304

commit v2 on v1

--- a/solution.py
+++ b/solution.py
@@ -27,8 +27,8 @@
     n_r, n_c, supers, width, rows_dev, block_size,
     sig_ref, a_ref, d_ref, pat_ref,
     off_ref, diag_ref,
-    ag, ta, dfull, pbuf, rbuf, sbuf, rbuf2, left, right, goth, gown, grecv, hx, hrecv, zs, zrecv, res, tout, toff,
-    send_sems, s_ag, s_ta, s_d, s_p, s_p2, s_g, s_h, s_z, s_zag, s_xag, s_sib, s_off, local_sems,
+    ag, sig_t, sq, dfull, pbuf, rbuf, sbuf, rbuf2, left, right, goth, gown, grecv, hx, hrecv, zs, zrecv, res,
+    send_sems, s_ag, s_sq, s_d, s_p, s_p2, s_g, s_h, s_z, s_zag, s_xag, s_sib, local_sems,
 ):
     r = lax.axis_index("row")
     c = lax.axis_index("col")
@@ -65,17 +65,30 @@
     for dx in range(1, n_x):
         sig(2 * ((x + dx) % n_x) + k, c)
 
-    @pl.when(r != c)
-    def _():
-        sig(c, r)
-        pl.semaphore_wait(barrier, n_c + n_x)
-
-    @pl.when(r == c)
-    def _():
-        pl.semaphore_wait(barrier, n_c + n_x - 1)
-
-    for dc in range(1, n_c):
-        rcopy(a_ref, ag.at[c], s_ag.at[c], r, (c + dc) % n_c)
+    pl.semaphore_wait(barrier, n_c + n_x - 1)
+
+    n_line = 70
+    def line_copy(src, j, d, to):
+        slot = n_line + 2 * d + (1 if to > 0 else 0)
+        return pltpu.make_async_remote_copy(
+            src_ref=src, dst_ref=ag.at[j], send_sem=send_sems.at[slot], recv_sem=s_ag.at[j],
+            device_id={"row": r, "col": (c + to + n_c) % n_c}, device_id_type=pl.DeviceIdType.MESH,
+        )
+
+    def line(d, to, f):
+        for cc in range(n_c):
+            j = cc - to * d
+            if 0 <= j < n_c:
+                @pl.when(c == cc)
+                def _():
+                    f(j, 0 <= cc + to < n_c)
+
+    def start_own(j, onward, to):
+        if onward:
+            line_copy(a_ref, j, 0, to).start()
+
+    for to in (1, -1):
+        line(0, to, functools.partial(start_own, to=to))
     d_slice = lambda ref, rr: ref.at[:, pl.ds(rr * piece, width - rr * piece), pl.ds(rr * piece, piece)]
     d_src = lambda rr: d_ref.at[:, pl.ds(rr * piece, width - rr * piece), :]
 
@@ -96,21 +109,12 @@
     own_copy = pltpu.make_async_copy(a_ref, ag.at[c], local_sems.at[1])
     own_copy.start()
 
-    def ta_copy():
-        return pltpu.make_async_remote_copy(
-            src_ref=a_ref, dst_ref=ta, send_sem=send_sems.at[n_fixed - 1], recv_sem=s_ta.at[0],
-            device_id={"row": c, "col": r}, device_id_type=pl.DeviceIdType.MESH,
-        )
-
-    ta_local = lambda: pltpu.make_async_copy(a_ref, ta, s_ta.at[0])
-
-    @pl.when(r != c)
-    def _():
-        ta_copy().start()
-
-    @pl.when(r == c)
-    def _():
-        ta_local().start()
+    sig_t[...] = jnp.transpose(sig_ref[...])
+    sig_rows = lambda j: pl.ds(pl.multiple_of(j * rows_dev, SUBLANES), rows_dev)
+    for dc in range(1, n_c):
+        j = (c + dc) % n_c
+        rcopy(sig_t.at[sig_rows(j), :], sq.at[c], s_sq.at[c], r, j)
+    sq[c] = sig_t[sig_rows(c), :]
 
     for rr in range(1, n_r):
         dfull[:, 0 : rr * piece, rr * piece : (rr + 1) * piece] = jnp.zeros((supers, rr * piece, piece), jnp.float32)
@@ -123,7 +127,14 @@
             m = jnp.where(inside, pat_ref[s, b].astype(jnp.float32), m)
         return m
 
-    sigma_t = split(jnp.transpose(sig_ref[...]))
+    def pass_line(j, onward, to, d):
+        wait_recv(ag.at[j], s_ag.at[j])
+        if onward:
+            line_copy(ag.at[j], j, d, to).start()
+
+    for d in range(1, n_c):
+        for to in (1, -1):
+            line(d, to, functools.partial(pass_line, to=to, d=d))
 
     for rr in range(n_r):
         @pl.when((rr % 2 == k) & (rr // 2 != x))
@@ -134,12 +145,13 @@
     own_copy.wait()
     for dc in range(1, n_c):
         j = (c + dc) % n_c
-        wait_recv(ag.at[j], s_ag.at[j])
+        wait_recv(sq.at[j], s_sq.at[j])
+    sigma_rows = split(sq[...].reshape(n_r * rows_dev, block_rows))
 
     for s in range(supers):
         cols = slice(s * width, (s + 1) * width)
         block = ag[:, :, cols].reshape(block_rows, width) * mask_of(r * block_rows, block_rows, s)
-        part = dot3(sigma_t, split(block))
+        part = dot3(sigma_rows, split(block))
         pbuf[:, :, cols] = part.reshape(n_r, rows_dev, width)
     for i in range(n_x):
         xo = (x + 1 + i) % n_x
@@ -153,8 +165,6 @@
         @pl.when(r == rr)
         def _():
             pltpu.make_async_copy(d_src(rr), d_slice(dfull, rr), local_sems.at[0]).wait()
-
-    wait_recv(ta, s_ta.at[0])
 
     for i in range(n_x):
         xo = (x + 1 + i) % n_x
@@ -163,7 +173,7 @@
         if i < n_x - 1:
             rcopy(sbuf.at[xo], rbuf2.at[x], s_p2.at[x], 2 * xo + k, c)
 
-    t_first = (c * n_c + r) * rows_dev
+    t_first = (r * n_c + c) * rows_dev
     own_first = (r * n_c + c) * share
     masks = [mask_of(t_first, rows_dev, s) for s in range(supers)]
     step = 2 * LANES
@@ -177,7 +187,7 @@
     for s in range(supers):
         def store_scaled(j, v):
             left[s, 0:rows_dev, j : j + step] = -v
-        times_d(ta[:, s * width : (s + 1) * width] * masks[s], s, store_scaled)
+        times_d(a_ref[:, s * width : (s + 1) * width] * masks[s], s, store_scaled)
         own = dfull[s, pl.ds(pl.multiple_of(own_first, SUBLANES), share), :]
         left[s, rows_dev:, :] = own
         right[s, rows_dev:, :] = own
@@ -192,7 +202,7 @@
             y = y + rbuf2[(x + dx) % n_x, :, cols]
         def store_off(j, v):
             right[s, 0:rows_dev, j : j + step] = v
-            tout[:, s * width + j : s * width + j + step] = v
+            off_ref[:, s * width + j : s * width + j + step] = v
         times_d(y * (-masks[s]), s, store_off)
 
     def diag_part(s, dst):
@@ -208,14 +218,6 @@
 
     diag_part(1 - k, goth)
     rcopy(goth, grecv, s_g.at[0], sib, c)
-
-    def off_copy():
-        return pltpu.make_async_remote_copy(
-            src_ref=tout, dst_ref=toff, send_sem=send_sems.at[n_fixed - 2], recv_sem=s_off.at[0],
-            device_id={"row": c, "col": r}, device_id_type=pl.DeviceIdType.MESH,
-        )
-
-    off_local = lambda: pltpu.make_async_copy(tout, toff, s_off.at[0])
 
     diag_part(k, gown)
     wait_recv(grecv, s_g.at[0])
@@ -240,14 +242,6 @@
         if i < n_c - 1:
             rcopy(zs.at[j], zrecv.at[c], s_z.at[c], r, j)
 
-    @pl.when(r != c)
-    def _():
-        off_copy().start()
-
-    @pl.when(r == c)
-    def _():
-        off_local().start()
-
     total = zs[c]
     for dc in range(1, n_c):
         j = (c + dc) % n_c
@@ -276,9 +270,6 @@
             wait_recv(chunk, s_xag.at[xo * n_c + j])
             rcopy(chunk, chunk, s_sib.at[xo * n_c + j], sib, c)
 
-    wait_recv(toff, s_off.at[0])
-    off_ref[...] = toff[...]
-
     def expand(s):
         b = 0
         for i in range(nb):
@@ -308,10 +299,13 @@
         def _():
             d_copy(d_slice(dfull, rr), rr, n_fixed + n_x + rr // 2, sib).wait_send()
 
-    @pl.when(r != c)
-    def _():
-        ta_copy().wait_send()
-        off_copy().wait_send()
+    def sent(j, onward, to, d):
+        if onward:
+            line_copy(a_ref, j, d, to).wait_send()
+
+    for d in range(n_c):
+        for to in (1, -1):
+            line(d, to, functools.partial(sent, to=to, d=d))
 
 
 def fused_body(sigma_anc, anc_factor, diag_inverse, pattern):
@@ -338,7 +332,8 @@
         out_specs=(vm, vm),
         scratch_shapes=[
             f32(n_c, rows_dev, flat),
-            f32(rows_dev, flat),
+            f32(n_r * rows_dev, n_c * rows_dev),
+            f32(n_c, rows_dev, n_c * rows_dev),
             f32(supers, width, width),
             f32(n_r, rows_dev, flat),
             f32(n_x, rows_dev, flat),
@@ -354,11 +349,9 @@
             f32(n_c, q, LANES),
             f32(n_c, q, LANES),
             f32(supers, half_rows, LANES),
-            f32(rows_dev, flat),
-            f32(rows_dev, flat),
-            dma(64 + 2 * n_x),
-            dma(n_c), dma(1), dma(n_r), dma(n_x), dma(n_x), dma(1), dma(n_x * n_c), dma(n_c), dma(n_c),
-            dma(n_x * n_c), dma(n_x * n_c), dma(1), dma(2),
+            dma(70 + 2 * n_c),
+            dma(n_c), dma(n_c), dma(n_r), dma(n_x), dma(n_x), dma(1), dma(n_x * n_c), dma(n_c), dma(n_c),
+            dma(n_x * n_c), dma(n_x * n_c), dma(2),
         ],
         compiler_params=pltpu.CompilerParams(
             collective_id=0, has_side_effects=True, vmem_limit_bytes=56 * 1024 * 1024

time: 81.6 us -> 69.9 us (0.86)
  the two profiles are of different devices: /device:TPU:25 before, /device:TPU:9 now
where the time goes in v2:
time: 69.9 us; the launch traced here: 69.7 us
  Pallas kernels  62.5 us (89%)
  local copies, waits for them, and re-layouts  6.48 us (9%)
    pallas_call x1, Pallas kernels, fused_body(): pl.pallas_call(functools.partial(fused_kernel, n_r, n_c, supers, width, r...  62.5 us
    unnamed x2, local copies, waits for them, and re-layouts  4.72 us
    reshape x1, local copies, waits for them, and re-layouts, fused_body(): return (off.reshape(anc_factor.shape), diag)  1.76 us

profile of v2, /device:TPU:9, one launch (start us, length us, event | category | flops | bytes accessed | tf_op | source)
XLA Modules:
  0.0 69.7 jit_solution(14264637597596321715)
XLA Ops:
  0.6 1.6 %copy.6 = f32[6,8,2,512]{3,1,2,0:T(8,128)} copy(f32[6,8,2,512]{3,2,1,0:T(2,128)} %bitcast.3) | data formatting | bytes 393216
  2.3 62.5 %shard_map.59 = (f32[48,1024]{1,0:T(8,128)}, f32[2,512,512]{2,1,0:T(8,128)}) custom-call(f32[192,192]{1,0:T(8,128)} %sig_ref.1, f32[48,1024]{1,0:T(8,128)} %bitcast.2, f32[2,512,128]{2,1,0:T(8,128)} %d_ref.1, s32[2,6]{1,0:T(2,128)} %pat_ref.1), custom_call_target="tpu_custom_call" | custom-call | tf_op jit(solution)/shard_map/pallas_call | solution.py:325
  64.8 1.8 %reshape.11 = f32[48,2,512]{2,1,0:T(2,128)} reshape(f32[48,1024]{1,0:T(8,128)} %get-tuple-element.4) | data formatting | bytes 393216 | tf_op jit(solution)/shard_map/reshape | solution.py:360
  66.6 3.1 %copy.8 = f32[2,512,512]{2,1,0:T(8,128)} copy(f32[2,512,512]{2,1,0:T(8,128)} %get-tuple-element.9) | data formatting | bytes 4194304

commit v3 on v2

--- a/solution.py
+++ b/solution.py
@@ -68,10 +68,13 @@
     pl.semaphore_wait(barrier, n_c + n_x - 1)
 
     n_line = 70
-    def line_copy(src, j, d, to):
-        slot = n_line + 2 * d + (1 if to > 0 else 0)
+    part_of = lambda j, h: ag.at[j, :, pl.ds(h * width, width)]
+    own_part = lambda h: a_ref.at[:, pl.ds(h * width, width)]
+
+    def line_copy(src, j, d, to, h):
+        slot = n_line + (2 * d + (1 if to > 0 else 0)) * supers + h
         return pltpu.make_async_remote_copy(
-            src_ref=src, dst_ref=ag.at[j], send_sem=send_sems.at[slot], recv_sem=s_ag.at[j],
+            src_ref=src, dst_ref=part_of(j, h), send_sem=send_sems.at[slot], recv_sem=s_ag.at[j * supers + h],
             device_id={"row": r, "col": (c + to + n_c) % n_c}, device_id_type=pl.DeviceIdType.MESH,
         )
 
@@ -83,12 +86,13 @@
                 def _():
                     f(j, 0 <= cc + to < n_c)
 
-    def start_own(j, onward, to):
+    def start_own(j, onward, to, h):
         if onward:
-            line_copy(a_ref, j, 0, to).start()
-
-    for to in (1, -1):
-        line(0, to, functools.partial(start_own, to=to))
+            line_copy(own_part(h), j, 0, to, h).start()
+
+    for h in range(supers):
+        for to in (1, -1):
+            line(0, to, functools.partial(start_own, to=to, h=h))
     d_slice = lambda ref, rr: ref.at[:, pl.ds(rr * piece, width - rr * piece), pl.ds(rr * piece, piece)]
     d_src = lambda rr: d_ref.at[:, pl.ds(rr * piece, width - rr * piece), :]
 
@@ -127,14 +131,15 @@
             m = jnp.where(inside, pat_ref[s, b].astype(jnp.float32), m)
         return m
 
-    def pass_line(j, onward, to, d):
-        wait_recv(ag.at[j], s_ag.at[j])
+    def pass_line(j, onward, to, d, h):
+        wait_recv(part_of(j, h), s_ag.at[j * supers + h])
         if onward:
-            line_copy(ag.at[j], j, d, to).start()
+            line_copy(part_of(j, h), j, d, to, h).start()
 
     for d in range(1, n_c):
-        for to in (1, -1):
-            line(d, to, functools.partial(pass_line, to=to, d=d))
+        for h in range(supers):
+            for to in (1, -1):
+                line(d, to, functools.partial(pass_line, to=to, d=d, h=h))
 
     for rr in range(n_r):
         @pl.when((rr % 2 == k) & (rr // 2 != x))
@@ -299,13 +304,14 @@
         def _():
             d_copy(d_slice(dfull, rr), rr, n_fixed + n_x + rr // 2, sib).wait_send()
 
-    def sent(j, onward, to, d):
+    def sent(j, onward, to, d, h):
         if onward:
-            line_copy(a_ref, j, d, to).wait_send()
+            line_copy(own_part(h), j, d, to, h).wait_send()
 
     for d in range(n_c):
-        for to in (1, -1):
-            line(d, to, functools.partial(sent, to=to, d=d))
+        for h in range(supers):
+            for to in (1, -1):
+                line(d, to, functools.partial(sent, to=to, d=d, h=h))
 
 
 def fused_body(sigma_anc, anc_factor, diag_inverse, pattern):
@@ -349,8 +355,8 @@
             f32(n_c, q, LANES),
             f32(n_c, q, LANES),
             f32(supers, half_rows, LANES),
-            dma(70 + 2 * n_c),
-            dma(n_c), dma(n_c), dma(n_r), dma(n_x), dma(n_x), dma(1), dma(n_x * n_c), dma(n_c), dma(n_c),
+            dma(70 + 2 * n_c * supers),
+            dma(n_c * supers), dma(n_c), dma(n_r), dma(n_x), dma(n_x), dma(1), dma(n_x * n_c), dma(n_c), dma(n_c),
             dma(n_x * n_c), dma(n_x * n_c), dma(2),
         ],
         compiler_params=pltpu.CompilerParams(

time: 69.9 us -> 69.1 us (0.989)
  Pallas kernels: 62.5 us -> 61.7 us
    pallas_call x1, Pallas kernels: 62.5 us -> 61.7 us  [fused_body(): pl.pallas_call(functools.partial(fused_kernel, n_r, n_c, supers, width, r...]
where the time goes in v3:
time: 69.1 us; the launch traced here: 68.8 us
  Pallas kernels  61.7 us (89%)
  local copies, waits for them, and re-layouts  6.48 us (9%)
    pallas_call x1, Pallas kernels, fused_body(): pl.pallas_call(functools.partial(fused_kernel, n_r, n_c, supers, width, r...  61.7 us
    unnamed x2, local copies, waits for them, and re-layouts  4.72 us
    reshape x1, local copies, waits for them, and re-layouts, fused_body(): return (off.reshape(anc_factor.shape), diag)  1.76 us

profile of v3, /device:TPU:9, one launch (start us, length us, event | category | flops | bytes accessed | tf_op | source)
XLA Modules:
  0.0 68.8 jit_solution(18198193782254563526)
XLA Ops:
  0.6 1.6 %copy.6 = f32[6,8,2,512]{3,1,2,0:T(8,128)} copy(f32[6,8,2,512]{3,2,1,0:T(2,128)} %bitcast.3) | data formatting | bytes 393216
  2.3 61.7 %shard_map.59 = (f32[48,1024]{1,0:T(8,128)}, f32[2,512,512]{2,1,0:T(8,128)}) custom-call(f32[192,192]{1,0:T(8,128)} %sig_ref.1, f32[48,1024]{1,0:T(8,128)} %bitcast.2, f32[2,512,128]{2,1,0:T(8,128)} %d_ref.1, s32[2,6]{1,0:T(2,128)} %pat_ref.1), custom_call_target="tpu_custom_call" | custom-call | tf_op jit(solution)/shard_map/pallas_call | solution.py:331
  64.0 1.8 %reshape.11 = f32[48,2,512]{2,1,0:T(2,128)} reshape(f32[48,1024]{1,0:T(8,128)} %get-tuple-element.4) | data formatting | bytes 393216 | tf_op jit(solution)/shard_map/reshape | solution.py:366
  65.8 3.1 %copy.8 = f32[2,512,512]{2,1,0:T(8,128)} copy(f32[2,512,512]{2,1,0:T(8,128)} %get-tuple-element.9) | data formatting | bytes 4194304
